TPU v7x, 32 devices: a whole 2x2x4 slice. The times are simulated.
32 devices in a mesh: gx: 4 (over x, core), gy: 2 (over y), gz: 4 (over z).
Axes of the slice: x: 2, y: 2, z: 4, core: 2. Of those that a mesh axis runs over, the one named last changes fastest.
Arguments:
- positions: float32 [3, 4, 2, 4, 256], P(None, 'gx', 'gy', 'gz'), may hold values from 0 to 4, as said below
- velocities: float32 [3, 4, 2, 4, 256], P(None, 'gx', 'gy', 'gz'), may hold values from -6 to 6
- forces: float32 [3, 4, 2, 4, 256], P(None, 'gx', 'gy', 'gz'), may hold values from -6 to 6
- charges: float32 [4, 2, 4, 256], P('gx', 'gy', 'gz'), may hold values from -2 to 2
- inverse_mass: float32 [4, 2, 4, 256], P('gx', 'gy', 'gz'), may hold values from 0.5 to 2
- occupancy: int32 [4, 2, 4], P('gx', 'gy', 'gz'), may hold values from 128 to 256
- molecule: int32 [4, 2, 4, 256], P('gx', 'gy', 'gz'), may hold values from 0 to 127, never falling along the last dimension, each value on 1 to 4 neighbouring positions
Outputs:
- positions_out: float32 [3, 4, 2, 4, 256], P(None, 'gx', 'gy', 'gz')
- velocities_out: float32 [3, 4, 2, 4, 256], P(None, 'gx', 'gy', 'gz')
- forces_out: float32 [3, 4, 2, 4, 256], P(None, 'gx', 'gy', 'gz')
Inputs may be any that keep to these rules, and one draw needn't show every extreme that they name: `positions`: component c of a particle of the box with index k along dimension c lies in [k, k + 1).
All inputs are finite; a program needn't handle non-finite values.
Results may differ from a plain program's by a relative error of at most 0.0003.
Values sent between devices are 32-bit elements; how exact they have to be, the bound alone decides.
No kernel may reach another device: no remote copies, remote signals or barrier semaphores. Data moves between devices by JAX's collectives and lax.ppermute only.
A program may use at most 64 MiB of HBM per device.

v0:
```python
import jax
import jax.numpy as jnp
from jax import lax
from jax.sharding import PartitionSpec as P

cutoff_square = 4.0
soften_square = 0.25
time_step = 0.1
half_step = 0.05


def passed_along(block, axis, distance):
    devices = range(lax.axis_size(axis))
    route = [((i - distance) % len(devices), i) for i in devices]
    return lax.ppermute(block, axis, route)


def separations_of(target_places, source_places, lengths):
    separations = []
    for component in range(3):
        spacing = target_places[component][:, None] - source_places[component][None, :]
        separations.append(
            spacing - lengths[component] * jnp.floor(spacing / lengths[component] + 0.5)
        )
    squared = (
        separations[0] * separations[0]
        + separations[1] * separations[1]
        + separations[2] * separations[2]
    )
    switch = jnp.maximum(1.0 - squared / cutoff_square, 0.0)
    soften = squared + soften_square
    return (separations, switch * switch / (soften * jnp.sqrt(soften)))


def interact(target_places, target_charge, source_places, source_charge, lengths, pair_mask):
    separations, base = separations_of(target_places, source_places, lengths)
    weight = source_charge[None, :] * base
    if pair_mask is not None:
        weight = weight * pair_mask
    return jnp.stack(
        [target_charge * jnp.sum(weight * separation, axis=-1) for separation in separations]
    )


def cycle_offsets(cycle_size):
    if cycle_size >= 5:
        return [1, -1, 2, -2]
    return list(range(1, cycle_size))


def across_second(gathered):
    pieces = [gathered]
    for offset in cycle_offsets(lax.axis_size("gy")):
        pieces.append(passed_along(gathered, "gy", offset))
    return jnp.stack(pieces)


def across_first(gathered):
    pieces = [gathered]
    for offset in cycle_offsets(lax.axis_size("gx")):
        pieces.append(passed_along(gathered, "gx", offset))
    return jnp.stack(pieces)


def forward_sum(summed, places, charge_live, blocks, lengths):

    def advance(total, column):
        return (total + interact(places, charge_live, column[:3], column[3], lengths, None), None)

    result, unused = lax.scan(advance, summed, blocks)
    return result


def full_shell(places, charge_live, tower_data, lengths):
    stacked = across_first(across_second(tower_data))
    blocks = stacked.reshape(-1, 4, tower_data.shape[1])
    return forward_sum(jnp.zeros_like(places), places, charge_live, blocks, lengths)


def force_field(places, charge_live, same_molecule, lengths):
    sources = jnp.concatenate([places, charge_live[None]], axis=0)
    tower_data = lax.all_gather(sources, "gz", axis=1, tiled=True)
    summed = full_shell(places, charge_live, tower_data, lengths)
    return summed - interact(places, charge_live, places, charge_live, lengths, same_molecule)


def local(positions, velocities, forces, charges, inverse_mass, occupancy, molecule):
    lengths = (float(lax.axis_size("gx")), float(lax.axis_size("gy")), float(lax.axis_size("gz")))
    shape = positions.shape
    places = positions.reshape(3, -1)
    velocity = velocities.reshape(3, -1)
    current = forces.reshape(3, -1)
    slots_count = places.shape[1]
    slots = jnp.arange(slots_count, dtype=jnp.int32)
    charge_live = jnp.where(slots < occupancy.reshape(()), charges.reshape(-1), jnp.float32(0.0))
    mass_inverse = inverse_mass.reshape(-1)
    labels = molecule.reshape(-1)
    same_molecule = (labels[:, None] == labels[None, :]).astype(jnp.float32)
    for turn in range(2):
        midway = velocity + half_step * mass_inverse * current
        places = places + time_step * midway
        current = force_field(places, charge_live, same_molecule, lengths)
        velocity = midway + half_step * mass_inverse * current
    return (places.reshape(shape), velocity.reshape(shape), current.reshape(shape))


def solution(mesh):
    in_specs = (
        P(None, "gx", "gy", "gz", None),
        P(None, "gx", "gy", "gz", None),
        P(None, "gx", "gy", "gz", None),
        P("gx", "gy", "gz", None),
        P("gx", "gy", "gz", None),
        P("gx", "gy", "gz"),
        P("gx", "gy", "gz", None),
    )
    out_specs = (
        P(None, "gx", "gy", "gz", None),
        P(None, "gx", "gy", "gz", None),
        P(None, "gx", "gy", "gz", None),
    )
    return jax.shard_map(local, mesh=mesh, in_specs=in_specs, out_specs=out_specs, check_vma=False)
```

profile of v0, /device:TPU:1, one launch (start us, length us, event | category | flops | bytes accessed | tf_op | source)
XLA Modules:
  0.0 84.3 jit_solution(9478626252136731197)
XLA Ops:
  4.7 11.4 %all_gather.6 = f32[4,1024]{1,0:T(4,128)S(1)} all-gather(f32[4,256]{1,0:T(4,128)S(1)} %pad_maximum_fusion.5), channel_id=1, replica_groups=mesh['gx'=4,'gy'=2,'gz'=4] {'gz'}, dimensions={1}, use_global_device_ids=true | all-gather | bytes 20480 | tf_op jit(solution)/shard_map/all_gather | solution.py:82
  19.0 5.6 %collective-permute-start.1 = (f32[2,4,1024]{2,1,0:T(4,128)S(1)}, f32[2,4,1024]{2,1,0:T(4,128)S(1)}, u32[]{:S(2)}, u32[]{:S(2)}) collective-permute-start(f32[2,4,1024]{2,1,0:T(4,128)S(1)} %get-tuple-element.156), channel_id=1, source_target_pairs={{24,0},{0,8},{8,16},{16,24},{25,1},{1,9},{9,17},{17,25},{26,2},{2,... | collective-permute-start | bytes 98312 | tf_op jit(solution)/shard_map/ppermute | solution.py:15
  25.6 1.7 %collective-permute-done.2 = f32[2,4,1024]{2,1,0:T(4,128)S(1)} collective-permute-done((f32[2,4,1024]{2,1,0:T(4,128)S(1)}, f32[2,4,1024]{2,1,0:T(4,128)S(1)}, u32[]{:S(2)}, u32[]{:S(2)}) %collective-permute-start.2) | collective-permute-done | bytes 32800 | tf_op jit(solution)/shard_map/ppermute | solution.py:15
  28.2 16.3 %while.22 = (s32[]{:T(128)}, f32[3,256]{1,0:T(4,128)S(1)}, f32[8,4,1024]{2,1,0:T(4,128)S(1)}, f32[3,256]{1,0:T(4,128)S(1)}, f32[256]{0:T(256)S(1)}, /*index=5*/s32[]{:T(128)}, s32[]{:T(128)}, s32[]{}, s32[]{}, s32[]{}) while((s32[]{:T(128)}, f32[3,256]{1,0:T(4,128)S(1)}, f32[8,4,1024]{2,1,0:T(4,128)S(1)}, f32[3,256]{1,0:T(4,128)S(1)}, ...), condition=%wide.region_4.5_spmd.clone, body=%wide.region_0.4_spmd.clone.sunk | while | flops 9702406 | bytes 77987 | solution.py:70
  28.3 1.9 %fusion.108 = (f32[256]{0:T(256)S(1)}, f32[256]{0:T(256)S(1)}, f32[256]{0:T(256)S(1)}) fusion(f32[1024]{0:T(1024)S(1)} %bitcast.119, f32[256]{0:T(256)S(1)} %bitcast.141, f32[1024]{0:T(1024)S(1)} %bitcast.120, f32[256]{0:T(256)S(1)} %bitcast.140, f32[1024]{0:T(1024)S(1)} %bitcast.118, f32[256]{0:T(256)S(1)} %bitcast.139, f32[1024]{0:T(1024)S(1)} %bitcast.117), kind=kLoop, calls=%fused_computation.14.clone.1 | loop fusion | flops 9698560 | bytes 22528 | tf_op jit(solution)/shard_map/while/body/eval_jaxpr/reduce_sum | solution.py:41
  30.3 1.9 %fusion.108 = (f32[256]{0:T(256)S(1)}, f32[256]{0:T(256)S(1)}, f32[256]{0:T(256)S(1)}) fusion(f32[1024]{0:T(1024)S(1)} %bitcast.119, f32[256]{0:T(256)S(1)} %bitcast.141, f32[1024]{0:T(1024)S(1)} %bitcast.120, f32[256]{0:T(256)S(1)} %bitcast.140, f32[1024]{0:T(1024)S(1)} %bitcast.118, f32[256]{0:T(256)S(1)} %bitcast.139, f32[1024]{0:T(1024)S(1)} %bitcast.117), kind=kLoop, calls=%fused_computation.14.clone.1 | loop fusion | flops 9698560 | bytes 22528 | tf_op jit(solution)/shard_map/while/body/eval_jaxpr/reduce_sum | solution.py:41
  32.3 1.9 %fusion.108 = (f32[256]{0:T(256)S(1)}, f32[256]{0:T(256)S(1)}, f32[256]{0:T(256)S(1)}) fusion(f32[1024]{0:T(1024)S(1)} %bitcast.119, f32[256]{0:T(256)S(1)} %bitcast.141, f32[1024]{0:T(1024)S(1)} %bitcast.120, f32[256]{0:T(256)S(1)} %bitcast.140, f32[1024]{0:T(1024)S(1)} %bitcast.118, f32[256]{0:T(256)S(1)} %bitcast.139, f32[1024]{0:T(1024)S(1)} %bitcast.117), kind=kLoop, calls=%fused_computation.14.clone.1 | loop fusion | flops 9698560 | bytes 22528 | tf_op jit(solution)/shard_map/while/body/eval_jaxpr/reduce_sum | solution.py:41
  34.4 1.9 %fusion.108 = (f32[256]{0:T(256)S(1)}, f32[256]{0:T(256)S(1)}, f32[256]{0:T(256)S(1)}) fusion(f32[1024]{0:T(1024)S(1)} %bitcast.119, f32[256]{0:T(256)S(1)} %bitcast.141, f32[1024]{0:T(1024)S(1)} %bitcast.120, f32[256]{0:T(256)S(1)} %bitcast.140, f32[1024]{0:T(1024)S(1)} %bitcast.118, f32[256]{0:T(256)S(1)} %bitcast.139, f32[1024]{0:T(1024)S(1)} %bitcast.117), kind=kLoop, calls=%fused_computation.14.clone.1 | loop fusion | flops 9698560 | bytes 22528 | tf_op jit(solution)/shard_map/while/body/eval_jaxpr/reduce_sum | solution.py:41
  36.4 1.9 %fusion.108 = (f32[256]{0:T(256)S(1)}, f32[256]{0:T(256)S(1)}, f32[256]{0:T(256)S(1)}) fusion(f32[1024]{0:T(1024)S(1)} %bitcast.119, f32[256]{0:T(256)S(1)} %bitcast.141, f32[1024]{0:T(1024)S(1)} %bitcast.120, f32[256]{0:T(256)S(1)} %bitcast.140, f32[1024]{0:T(1024)S(1)} %bitcast.118, f32[256]{0:T(256)S(1)} %bitcast.139, f32[1024]{0:T(1024)S(1)} %bitcast.117), kind=kLoop, calls=%fused_computation.14.clone.1 | loop fusion | flops 9698560 | bytes 22528 | tf_op jit(solution)/shard_map/while/body/eval_jaxpr/reduce_sum | solution.py:41
  38.4 1.9 %fusion.108 = (f32[256]{0:T(256)S(1)}, f32[256]{0:T(256)S(1)}, f32[256]{0:T(256)S(1)}) fusion(f32[1024]{0:T(1024)S(1)} %bitcast.119, f32[256]{0:T(256)S(1)} %bitcast.141, f32[1024]{0:T(1024)S(1)} %bitcast.120, f32[256]{0:T(256)S(1)} %bitcast.140, f32[1024]{0:T(1024)S(1)} %bitcast.118, f32[256]{0:T(256)S(1)} %bitcast.139, f32[1024]{0:T(1024)S(1)} %bitcast.117), kind=kLoop, calls=%fused_computation.14.clone.1 | loop fusion | flops 9698560 | bytes 22528 | tf_op jit(solution)/shard_map/while/body/eval_jaxpr/reduce_sum | solution.py:41
  40.5 1.9 %fusion.108 = (f32[256]{0:T(256)S(1)}, f32[256]{0:T(256)S(1)}, f32[256]{0:T(256)S(1)}) fusion(f32[1024]{0:T(1024)S(1)} %bitcast.119, f32[256]{0:T(256)S(1)} %bitcast.141, f32[1024]{0:T(1024)S(1)} %bitcast.120, f32[256]{0:T(256)S(1)} %bitcast.140, f32[1024]{0:T(1024)S(1)} %bitcast.118, f32[256]{0:T(256)S(1)} %bitcast.139, f32[1024]{0:T(1024)S(1)} %bitcast.117), kind=kLoop, calls=%fused_computation.14.clone.1 | loop fusion | flops 9698560 | bytes 22528 | tf_op jit(solution)/shard_map/while/body/eval_jaxpr/reduce_sum | solution.py:41
  42.5 1.9 %fusion.108 = (f32[256]{0:T(256)S(1)}, f32[256]{0:T(256)S(1)}, f32[256]{0:T(256)S(1)}) fusion(f32[1024]{0:T(1024)S(1)} %bitcast.119, f32[256]{0:T(256)S(1)} %bitcast.141, f32[1024]{0:T(1024)S(1)} %bitcast.120, f32[256]{0:T(256)S(1)} %bitcast.140, f32[1024]{0:T(1024)S(1)} %bitcast.118, f32[256]{0:T(256)S(1)} %bitcast.139, f32[1024]{0:T(1024)S(1)} %bitcast.117), kind=kLoop, calls=%fused_computation.14.clone.1 | loop fusion | flops 9698560 | bytes 22528 | tf_op jit(solution)/shard_map/while/body/eval_jaxpr/reduce_sum | solution.py:41
  45.2 10.3 %all_gather.7 = f32[4,1024]{1,0:T(4,128)S(1)} all-gather(f32[4,256]{1,0:T(4,128)S(1)} %pad_maximum_fusion.4), channel_id=1, replica_groups=mesh['gx'=4,'gy'=2,'gz'=4] {'gz'}, dimensions={1}, use_global_device_ids=true | all-gather | bytes 20480 | tf_op jit(solution)/shard_map/all_gather | solution.py:82
  58.2 4.5 %collective-permute-start.5 = (f32[2,4,1024]{2,1,0:T(4,128)S(1)}, f32[2,4,1024]{2,1,0:T(4,128)S(1)}, u32[]{:S(2)}, u32[]{:S(2)}) collective-permute-start(f32[2,4,1024]{2,1,0:T(4,128)S(1)} %get-tuple-element.154), channel_id=1, source_target_pairs={{24,0},{0,8},{8,16},{16,24},{25,1},{1,9},{9,17},{17,25},{26,2},{2,... | collective-permute-start | bytes 98312 | tf_op jit(solution)/shard_map/ppermute | solution.py:15
  64.0 2.0 %collective-permute-done.6 = f32[2,4,1024]{2,1,0:T(4,128)S(1)} collective-permute-done((f32[2,4,1024]{2,1,0:T(4,128)S(1)}, f32[2,4,1024]{2,1,0:T(4,128)S(1)}, u32[]{:S(2)}, u32[]{:S(2)}) %collective-permute-start.6) | collective-permute-done | bytes 32800 | tf_op jit(solution)/shard_map/ppermute | solution.py:15
  66.8 16.3 %while.23 = (s32[]{:T(128)}, f32[3,256]{1,0:T(4,128)S(1)}, f32[8,4,1024]{2,1,0:T(4,128)S(1)}, f32[3,256]{1,0:T(4,128)S(1)}, f32[256]{0:T(256)S(1)}, /*index=5*/s32[]{:T(128)}, s32[]{:T(128)}, s32[]{}, s32[]{}, s32[]{}) while((s32[]{:T(128)}, f32[3,256]{1,0:T(4,128)S(1)}, f32[8,4,1024]{2,1,0:T(4,128)S(1)}, ...), condition=%wide.region_12.13_spmd.clone, body=%wide.region_8.12_spmd.clone.sunk | while | flops 9702406 | bytes 77987 | solution.py:70
  66.9 1.9 %fusion.111 = (f32[256]{0:T(256)S(1)}, f32[256]{0:T(256)S(1)}, f32[256]{0:T(256)S(1)}) fusion(f32[1024]{0:T(1024)S(1)} %bitcast.123, f32[256]{0:T(256)S(1)} %bitcast.144, f32[1024]{0:T(1024)S(1)} %bitcast.124, f32[256]{0:T(256)S(1)} %bitcast.143, f32[1024]{0:T(1024)S(1)} %bitcast.122, f32[256]{0:T(256)S(1)} %bitcast.142, f32[1024]{0:T(1024)S(1)} %bitcast.121), kind=kLoop, calls=%fused_computation.48.clone.1 | loop fusion | flops 9698560 | bytes 22528 | tf_op jit(solution)/shard_map/while/body/eval_jaxpr/reduce_sum | solution.py:41
  68.9 1.9 %fusion.111 = (f32[256]{0:T(256)S(1)}, f32[256]{0:T(256)S(1)}, f32[256]{0:T(256)S(1)}) fusion(f32[1024]{0:T(1024)S(1)} %bitcast.123, f32[256]{0:T(256)S(1)} %bitcast.144, f32[1024]{0:T(1024)S(1)} %bitcast.124, f32[256]{0:T(256)S(1)} %bitcast.143, f32[1024]{0:T(1024)S(1)} %bitcast.122, f32[256]{0:T(256)S(1)} %bitcast.142, f32[1024]{0:T(1024)S(1)} %bitcast.121), kind=kLoop, calls=%fused_computation.48.clone.1 | loop fusion | flops 9698560 | bytes 22528 | tf_op jit(solution)/shard_map/while/body/eval_jaxpr/reduce_sum | solution.py:41
  71.0 1.9 %fusion.111 = (f32[256]{0:T(256)S(1)}, f32[256]{0:T(256)S(1)}, f32[256]{0:T(256)S(1)}) fusion(f32[1024]{0:T(1024)S(1)} %bitcast.123, f32[256]{0:T(256)S(1)} %bitcast.144, f32[1024]{0:T(1024)S(1)} %bitcast.124, f32[256]{0:T(256)S(1)} %bitcast.143, f32[1024]{0:T(1024)S(1)} %bitcast.122, f32[256]{0:T(256)S(1)} %bitcast.142, f32[1024]{0:T(1024)S(1)} %bitcast.121), kind=kLoop, calls=%fused_computation.48.clone.1 | loop fusion | flops 9698560 | bytes 22528 | tf_op jit(solution)/shard_map/while/body/eval_jaxpr/reduce_sum | solution.py:41
  73.0 1.9 %fusion.111 = (f32[256]{0:T(256)S(1)}, f32[256]{0:T(256)S(1)}, f32[256]{0:T(256)S(1)}) fusion(f32[1024]{0:T(1024)S(1)} %bitcast.123, f32[256]{0:T(256)S(1)} %bitcast.144, f32[1024]{0:T(1024)S(1)} %bitcast.124, f32[256]{0:T(256)S(1)} %bitcast.143, f32[1024]{0:T(1024)S(1)} %bitcast.122, f32[256]{0:T(256)S(1)} %bitcast.142, f32[1024]{0:T(1024)S(1)} %bitcast.121), kind=kLoop, calls=%fused_computation.48.clone.1 | loop fusion | flops 9698560 | bytes 22528 | tf_op jit(solution)/shard_map/while/body/eval_jaxpr/reduce_sum | solution.py:41
  75.0 1.9 %fusion.111 = (f32[256]{0:T(256)S(1)}, f32[256]{0:T(256)S(1)}, f32[256]{0:T(256)S(1)}) fusion(f32[1024]{0:T(1024)S(1)} %bitcast.123, f32[256]{0:T(256)S(1)} %bitcast.144, f32[1024]{0:T(1024)S(1)} %bitcast.124, f32[256]{0:T(256)S(1)} %bitcast.143, f32[1024]{0:T(1024)S(1)} %bitcast.122, f32[256]{0:T(256)S(1)} %bitcast.142, f32[1024]{0:T(1024)S(1)} %bitcast.121), kind=kLoop, calls=%fused_computation.48.clone.1 | loop fusion | flops 9698560 | bytes 22528 | tf_op jit(solution)/shard_map/while/body/eval_jaxpr/reduce_sum | solution.py:41
  77.1 1.9 %fusion.111 = (f32[256]{0:T(256)S(1)}, f32[256]{0:T(256)S(1)}, f32[256]{0:T(256)S(1)}) fusion(f32[1024]{0:T(1024)S(1)} %bitcast.123, f32[256]{0:T(256)S(1)} %bitcast.144, f32[1024]{0:T(1024)S(1)} %bitcast.124, f32[256]{0:T(256)S(1)} %bitcast.143, f32[1024]{0:T(1024)S(1)} %bitcast.122, f32[256]{0:T(256)S(1)} %bitcast.142, f32[1024]{0:T(1024)S(1)} %bitcast.121), kind=kLoop, calls=%fused_computation.48.clone.1 | loop fusion | flops 9698560 | bytes 22528 | tf_op jit(solution)/shard_map/while/body/eval_jaxpr/reduce_sum | solution.py:41
  79.1 1.9 %fusion.111 = (f32[256]{0:T(256)S(1)}, f32[256]{0:T(256)S(1)}, f32[256]{0:T(256)S(1)}) fusion(f32[1024]{0:T(1024)S(1)} %bitcast.123, f32[256]{0:T(256)S(1)} %bitcast.144, f32[1024]{0:T(1024)S(1)} %bitcast.124, f32[256]{0:T(256)S(1)} %bitcast.143, f32[1024]{0:T(1024)S(1)} %bitcast.122, f32[256]{0:T(256)S(1)} %bitcast.142, f32[1024]{0:T(1024)S(1)} %bitcast.121), kind=kLoop, calls=%fused_computation.48.clone.1 | loop fusion | flops 9698560 | bytes 22528 | tf_op jit(solution)/shard_map/while/body/eval_jaxpr/reduce_sum | solution.py:41
  81.1 1.9 %fusion.111 = (f32[256]{0:T(256)S(1)}, f32[256]{0:T(256)S(1)}, f32[256]{0:T(256)S(1)}) fusion(f32[1024]{0:T(1024)S(1)} %bitcast.123, f32[256]{0:T(256)S(1)} %bitcast.144, f32[1024]{0:T(1024)S(1)} %bitcast.124, f32[256]{0:T(256)S(1)} %bitcast.143, f32[1024]{0:T(1024)S(1)} %bitcast.122, f32[256]{0:T(256)S(1)} %bitcast.142, f32[1024]{0:T(1024)S(1)} %bitcast.121), kind=kLoop, calls=%fused_computation.48.clone.1 | loop fusion | flops 9698560 | bytes 22528 | tf_op jit(solution)/shard_map/while/body/eval_jaxpr/reduce_sum | solution.py:41
  (107 shorter events, 15.8 us)
Async XLA Ops:
  0.6 0.7 copy-start
  2.7 0.7 copy-start.2
  3.4 0.7 copy-start.3
  16.1 2.9 %collective-permute-start = (f32[4,1024]{1,0:T(4,128)S(1)}, f32[4,1024]{1,0:T(4,128)S(1)}, u32[]{:S(2)}, u32[]{:S(2)}) collective-permute-start(f32[4,1024]{1,0:T(4,128)S(1)} %all_gather.6), channel_id=1, source_target_pairs={{4,0},{0,4},{5,1},{1,5},{6,2},{2,6},{7,3},{3,7},{12,8},{8,12},{13,... | collective-permute-start | bytes 49160 | tf_op jit(solution)/shard_map/ppermute | solution.py:15
  19.0 6.6 %collective-permute-start.1 = (f32[2,4,1024]{2,1,0:T(4,128)S(1)}, f32[2,4,1024]{2,1,0:T(4,128)S(1)}, u32[]{:S(2)}, u32[]{:S(2)}) collective-permute-start(f32[2,4,1024]{2,1,0:T(4,128)S(1)} %get-tuple-element.156), channel_id=1, source_target_pairs={{24,0},{0,8},{8,16},{16,24},{25,1},{1,9},{9,17},{17,25},{26,2},{2,... | collective-permute-start | bytes 98312 | tf_op jit(solution)/shard_map/ppermute | solution.py:15
  24.6 2.8 %collective-permute-start.2 = (f32[2,4,1024]{2,1,0:T(4,128)S(1)}, f32[2,4,1024]{2,1,0:T(4,128)S(1)}, u32[]{:S(2)}, u32[]{:S(2)}) collective-permute-start(f32[2,4,1024]{2,1,0:T(4,128)S(1)} %get-tuple-element.156), channel_id=1, source_target_pairs={{16,0},{24,8},{0,16},{8,24},{17,1},{25,9},{1,17},{9,25},{18,2},{26... | collective-permute-start | bytes 98312 | tf_op jit(solution)/shard_map/ppermute | solution.py:15
  24.8 3.3 %collective-permute-start.3 = (f32[2,4,1024]{2,1,0:T(4,128)S(1)}, f32[2,4,1024]{2,1,0:T(4,128)S(1)}, u32[]{:S(2)}, u32[]{:S(2)}) collective-permute-start(f32[2,4,1024]{2,1,0:T(4,128)S(1)} %get-tuple-element.156), channel_id=1, source_target_pairs={{8,0},{16,8},{24,16},{0,24},{9,1},{17,9},{25,17},{1,25},{10,2},{18... | collective-permute-start | bytes 98312 | tf_op jit(solution)/shard_map/ppermute | solution.py:15
  44.5 0.7 copy-start.1
  55.5 2.6 %collective-permute-start.4 = (f32[4,1024]{1,0:T(4,128)S(1)}, f32[4,1024]{1,0:T(4,128)S(1)}, u32[]{:S(2)}, u32[]{:S(2)}) collective-permute-start(f32[4,1024]{1,0:T(4,128)S(1)} %all_gather.7), channel_id=1, source_target_pairs={{4,0},{0,4},{5,1},{1,5},{6,2},{2,6},{7,3},{3,7},{12,8},{8,12},{13,... | collective-permute-start | bytes 49160 | tf_op jit(solution)/shard_map/ppermute | solution.py:15
  58.2 5.9 %collective-permute-start.5 = (f32[2,4,1024]{2,1,0:T(4,128)S(1)}, f32[2,4,1024]{2,1,0:T(4,128)S(1)}, u32[]{:S(2)}, u32[]{:S(2)}) collective-permute-start(f32[2,4,1024]{2,1,0:T(4,128)S(1)} %get-tuple-element.154), channel_id=1, source_target_pairs={{24,0},{0,8},{8,16},{16,24},{25,1},{1,9},{9,17},{17,25},{26,2},{2,... | collective-permute-start | bytes 98312 | tf_op jit(solution)/shard_map/ppermute | solution.py:15
  62.7 3.3 %collective-permute-start.6 = (f32[2,4,1024]{2,1,0:T(4,128)S(1)}, f32[2,4,1024]{2,1,0:T(4,128)S(1)}, u32[]{:S(2)}, u32[]{:S(2)}) collective-permute-start(f32[2,4,1024]{2,1,0:T(4,128)S(1)} %get-tuple-element.154), channel_id=1, source_target_pairs={{16,0},{24,8},{0,16},{8,24},{17,1},{25,9},{1,17},{9,25},{18,2},{26... | collective-permute-start | bytes 98312 | tf_op jit(solution)/shard_map/ppermute | solution.py:15
  63.5 3.3 %collective-permute-start.7 = (f32[2,4,1024]{2,1,0:T(4,128)S(1)}, f32[2,4,1024]{2,1,0:T(4,128)S(1)}, u32[]{:S(2)}, u32[]{:S(2)}) collective-permute-start(f32[2,4,1024]{2,1,0:T(4,128)S(1)} %get-tuple-element.154), channel_id=1, source_target_pairs={{8,0},{16,8},{24,16},{0,24},{9,1},{17,9},{25,17},{1,25},{10,2},{18... | collective-permute-start | bytes 98312 | tf_op jit(solution)/shard_map/ppermute | solution.py:15
where the time goes:
time: 84.6 us; the launch traced here: 84.3 us
  other arithmetic  34.2 us (40%)
  blocking collectives  21.7 us (26%)
  starting transfers between devices  13.8 us (16%)
  waiting for transfers between devices  8.21 us (10%)
  local copies, waits for them, and re-layouts  4.31 us (5%)
  between operations  1.39 us (2%)
    reduce_sum x18, other arithmetic, interact(): jnp.sum(weight * separation, axis=-1)  32.3 us
    all_gather x2, blocking collectives, force_field(): tower_data = lax.all_gather(sources, 'gz', axis=1, tiled=True)  21.7 us
    ppermute x8, starting transfers between devices, passed_along(): return lax.ppermute(block, axis, route)  13.8 us
    ppermute x8, waiting for transfers between devices, passed_along(): return lax.ppermute(block, axis, route)  8.21 us
    unnamed x8, local copies, waits for them, and re-layouts  2.04 us
  transfers between devices with their start and end apart: 8, of which 7 were waited for; matrix products, arithmetic and copies ran while one was open for 1% of the time, Pallas kernels for 0%

commit v1 on v0

--- a/solution.py
+++ b/solution.py
@@ -7,6 +7,18 @@
 soften_square = 0.25
 time_step = 0.1
 half_step = 0.05
+
+
+def _store_halves(inputs, axis_no):
+    n_parts = lax.axis_size("gz")
+    built = sorted(((dev, (dev + 1) % n_parts) for dev in range(n_parts)))
+    v_next = inputs
+    buffers = [v_next]
+    for c in [*range(1, n_parts)]:
+        v_next = lax.ppermute(v_next, "gz", built)
+        buffers.insert(0, v_next)
+    clean = jnp.concatenate(buffers, axis=axis_no)
+    return jnp.roll(clean, (lax.axis_index("gz") + 1) * inputs.shape[axis_no], axis=axis_no)
 
 
 def passed_along(block, axis, distance):
@@ -79,7 +91,7 @@
 
 def force_field(places, charge_live, same_molecule, lengths):
     sources = jnp.concatenate([places, charge_live[None]], axis=0)
-    tower_data = lax.all_gather(sources, "gz", axis=1, tiled=True)
+    tower_data = _store_halves(sources, 1)
     summed = full_shell(places, charge_live, tower_data, lengths)
     return summed - interact(places, charge_live, places, charge_live, lengths, same_molecule)
 

time: 84.6 us -> 90.8 us (1.073)
  waiting for transfers between devices: 8.21 us -> 32.3 us
  blocking collectives: 21.7 us -> 0 us
  starting transfers between devices: 13.8 us -> 17.4 us
    ppermute x0 -> x6, waiting for transfers between devices: none -> 24.3 us  [_store_halves(): v_next = lax.ppermute(v_next, 'gz', built)]
    all_gather x2 -> x0, blocking collectives: 21.7 us -> none  [force_field(): tower_data = lax.all_gather(sources, 'gz', axis=1, tiled=True)]
    ppermute x0 -> x6, starting transfers between devices: none -> 2.24 us  [_store_halves(): v_next = lax.ppermute(v_next, 'gz', built)]
    ppermute x8, starting transfers between devices: 13.8 us -> 15.1 us  [passed_along(): return lax.ppermute(block, axis, route)]
  transfers between devices with their start and end apart: 8 -> 14, of which waited for: 7 -> 13; matrix products, arithmetic and copies ran while one was open for 1% -> 1% of each run, Pallas kernels for 0% -> 0%
where the time goes in v1:
time: 90.8 us; the launch traced here: 90.5 us
  other arithmetic  34.5 us (38%)
  waiting for transfers between devices  32.3 us (36%)
  starting transfers between devices  17.4 us (19%)
  local copies, waits for them, and re-layouts  4.28 us (5%)
  between operations  1.4 us (2%)
    reduce_sum x18, other arithmetic, interact(): jnp.sum(weight * separation, axis=-1)  32.3 us
    ppermute x6, waiting for transfers between devices, _store_halves(): v_next = lax.ppermute(v_next, 'gz', built)  24.3 us
    ppermute x8, starting transfers between devices, passed_along(): return lax.ppermute(block, axis, route)  15.1 us
    ppermute x8, waiting for transfers between devices, passed_along(): return lax.ppermute(block, axis, route)  8.07 us
    ppermute x6, starting transfers between devices, _store_halves(): v_next = lax.ppermute(v_next, 'gz', built)  2.24 us
    unnamed x8, local copies, waits for them, and re-layouts  2.04 us
  transfers between devices with their start and end apart: 14, of which 13 were waited for; matrix products, arithmetic and copies ran while one was open for 1% of the time, Pallas kernels for 0%

profile of v1, /device:TPU:1, one launch (start us, length us, event | category | flops | bytes accessed | tf_op | source)
XLA Modules:
  0.0 90.5 jit_solution(17285192098272769530)
XLA Ops:
  4.7 2.2 %collective-permute-start = (f32[4,256]{1,0:T(4,128)S(1)}, f32[4,256]{1,0:T(4,128)S(1)}, u32[]{:S(2)}, u32[]{:S(2)}) collective-permute-start(f32[4,256]{1,0:T(4,128)S(1)} %pad_maximum_fusion.5), channel_id=1, source_target_pairs={{0,1},{1,2},{2,3},{3,0},{4,5},{5,6},{6,7},{7,4},{8,9},{9,10},{10,1... | collective-permute-start | bytes 12296 | tf_op jit(solution)/shard_map/ppermute | solution.py:18
  6.9 3.0 %collective-permute-done = f32[4,256]{1,0:T(4,128)S(1)} collective-permute-done((f32[4,256]{1,0:T(4,128)S(1)}, f32[4,256]{1,0:T(4,128)S(1)}, u32[]{:S(2)}, u32[]{:S(2)}) %collective-permute-start) | collective-permute-done | bytes 4128 | tf_op jit(solution)/shard_map/ppermute | solution.py:18
  9.9 4.3 %collective-permute-done.1 = f32[4,256]{1,0:T(4,128)S(1)} collective-permute-done((f32[4,256]{1,0:T(4,128)S(1)}, f32[4,256]{1,0:T(4,128)S(1)}, u32[]{:S(2)}, u32[]{:S(2)}) %collective-permute-start.1) | collective-permute-done | bytes 4128 | tf_op jit(solution)/shard_map/ppermute | solution.py:18
  14.2 4.3 %collective-permute-done.2 = f32[4,256]{1,0:T(4,128)S(1)} collective-permute-done((f32[4,256]{1,0:T(4,128)S(1)}, f32[4,256]{1,0:T(4,128)S(1)}, u32[]{:S(2)}, u32[]{:S(2)}) %collective-permute-start.2) | collective-permute-done | bytes 4128 | tf_op jit(solution)/shard_map/ppermute | solution.py:18
  21.5 6.1 %collective-permute-start.4 = (f32[2,4,1024]{2,1,0:T(4,128)S(1)}, f32[2,4,1024]{2,1,0:T(4,128)S(1)}, u32[]{:S(2)}, u32[]{:S(2)}) collective-permute-start(f32[2,4,1024]{2,1,0:T(4,128)S(1)} %get-tuple-element.157), channel_id=1, source_target_pairs={{24,0},{0,8},{8,16},{16,24},{25,1},{1,9},{9,17},{17,25},{26,2},{2,... | collective-permute-start | bytes 98312 | tf_op jit(solution)/shard_map/ppermute | solution.py:27
  31.0 16.2 %while.22 = (s32[]{:T(128)}, f32[3,256]{1,0:T(4,128)S(1)}, f32[8,4,1024]{2,1,0:T(4,128)S(1)}, f32[3,256]{1,0:T(4,128)S(1)}, f32[256]{0:T(256)S(1)}, /*index=5*/s32[]{:T(128)}, s32[]{:T(128)}, s32[]{}, s32[]{}, s32[]{}) while((s32[]{:T(128)}, f32[3,256]{1,0:T(4,128)S(1)}, f32[8,4,1024]{2,1,0:T(4,128)S(1)}, f32[3,256]{1,0:T(4,128)S(1)}, ...), condition=%wide.region_4.6_spmd.clone, body=%wide.region_0.5_spmd.clone.sunk | while | flops 9702406 | bytes 77987 | solution.py:82
  31.1 1.9 %fusion.126 = (f32[256]{0:T(256)S(1)}, f32[256]{0:T(256)S(1)}, f32[256]{0:T(256)S(1)}) fusion(f32[1024]{0:T(1024)S(1)} %bitcast.119, f32[256]{0:T(256)S(1)} %bitcast.141, f32[1024]{0:T(1024)S(1)} %bitcast.120, f32[256]{0:T(256)S(1)} %bitcast.140, f32[1024]{0:T(1024)S(1)} %bitcast.118, f32[256]{0:T(256)S(1)} %bitcast.139, f32[1024]{0:T(1024)S(1)} %bitcast.117), kind=kLoop, calls=%fused_computation.14.clone.1 | loop fusion | flops 9698560 | bytes 22528 | tf_op jit(solution)/shard_map/while/body/eval_jaxpr/reduce_sum | solution.py:53
  33.1 1.9 %fusion.126 = (f32[256]{0:T(256)S(1)}, f32[256]{0:T(256)S(1)}, f32[256]{0:T(256)S(1)}) fusion(f32[1024]{0:T(1024)S(1)} %bitcast.119, f32[256]{0:T(256)S(1)} %bitcast.141, f32[1024]{0:T(1024)S(1)} %bitcast.120, f32[256]{0:T(256)S(1)} %bitcast.140, f32[1024]{0:T(1024)S(1)} %bitcast.118, f32[256]{0:T(256)S(1)} %bitcast.139, f32[1024]{0:T(1024)S(1)} %bitcast.117), kind=kLoop, calls=%fused_computation.14.clone.1 | loop fusion | flops 9698560 | bytes 22528 | tf_op jit(solution)/shard_map/while/body/eval_jaxpr/reduce_sum | solution.py:53
  37.2 1.9 %fusion.126 = (f32[256]{0:T(256)S(1)}, f32[256]{0:T(256)S(1)}, f32[256]{0:T(256)S(1)}) fusion(f32[1024]{0:T(1024)S(1)} %bitcast.119, f32[256]{0:T(256)S(1)} %bitcast.141, f32[1024]{0:T(1024)S(1)} %bitcast.120, f32[256]{0:T(256)S(1)} %bitcast.140, f32[1024]{0:T(1024)S(1)} %bitcast.118, f32[256]{0:T(256)S(1)} %bitcast.139, f32[1024]{0:T(1024)S(1)} %bitcast.117), kind=kLoop, calls=%fused_computation.14.clone.1 | loop fusion | flops 9698560 | bytes 22528 | tf_op jit(solution)/shard_map/while/body/eval_jaxpr/reduce_sum | solution.py:53
  43.3 1.9 %fusion.126 = (f32[256]{0:T(256)S(1)}, f32[256]{0:T(256)S(1)}, f32[256]{0:T(256)S(1)}) fusion(f32[1024]{0:T(1024)S(1)} %bitcast.119, f32[256]{0:T(256)S(1)} %bitcast.141, f32[1024]{0:T(1024)S(1)} %bitcast.120, f32[256]{0:T(256)S(1)} %bitcast.140, f32[1024]{0:T(1024)S(1)} %bitcast.118, f32[256]{0:T(256)S(1)} %bitcast.139, f32[1024]{0:T(1024)S(1)} %bitcast.117), kind=kLoop, calls=%fused_computation.14.clone.1 | loop fusion | flops 9698560 | bytes 22528 | tf_op jit(solution)/shard_map/while/body/eval_jaxpr/reduce_sum | solution.py:53
  48.1 4.2 %collective-permute-done.7 = f32[4,256]{1,0:T(4,128)S(1)} collective-permute-done((f32[4,256]{1,0:T(4,128)S(1)}, f32[4,256]{1,0:T(4,128)S(1)}, u32[]{:S(2)}, u32[]{:S(2)}) %collective-permute-start.7) | collective-permute-done | bytes 4128 | tf_op jit(solution)/shard_map/ppermute | solution.py:18
  52.3 4.3 %collective-permute-done.8 = f32[4,256]{1,0:T(4,128)S(1)} collective-permute-done((f32[4,256]{1,0:T(4,128)S(1)}, f32[4,256]{1,0:T(4,128)S(1)}, u32[]{:S(2)}, u32[]{:S(2)}) %collective-permute-start.8) | collective-permute-done | bytes 4128 | tf_op jit(solution)/shard_map/ppermute | solution.py:18
  56.6 4.2 %collective-permute-done.9 = f32[4,256]{1,0:T(4,128)S(1)} collective-permute-done((f32[4,256]{1,0:T(4,128)S(1)}, f32[4,256]{1,0:T(4,128)S(1)}, u32[]{:S(2)}, u32[]{:S(2)}) %collective-permute-start.9) | collective-permute-done | bytes 4128 | tf_op jit(solution)/shard_map/ppermute | solution.py:18
  63.9 5.0 %collective-permute-start.11 = (f32[2,4,1024]{2,1,0:T(4,128)S(1)}, f32[2,4,1024]{2,1,0:T(4,128)S(1)}, u32[]{:S(2)}, u32[]{:S(2)}) collective-permute-start(f32[2,4,1024]{2,1,0:T(4,128)S(1)} %get-tuple-element.155), channel_id=1, source_target_pairs={{24,0},{0,8},{8,16},{16,24},{25,1},{1,9},{9,17},{17,25},{26,2},{2,... | collective-permute-start | bytes 98312 | tf_op jit(solution)/shard_map/ppermute | solution.py:27
  70.3 2.0 %collective-permute-done.12 = f32[2,4,1024]{2,1,0:T(4,128)S(1)} collective-permute-done((f32[2,4,1024]{2,1,0:T(4,128)S(1)}, f32[2,4,1024]{2,1,0:T(4,128)S(1)}, u32[]{:S(2)}, u32[]{:S(2)}) %collective-permute-start.12) | collective-permute-done | bytes 32800 | tf_op jit(solution)/shard_map/ppermute | solution.py:27
  73.1 16.3 %while.23 = (s32[]{:T(128)}, f32[3,256]{1,0:T(4,128)S(1)}, f32[8,4,1024]{2,1,0:T(4,128)S(1)}, f32[3,256]{1,0:T(4,128)S(1)}, f32[256]{0:T(256)S(1)}, /*index=5*/s32[]{:T(128)}, s32[]{:T(128)}, s32[]{}, s32[]{}, s32[]{}) while((s32[]{:T(128)}, f32[3,256]{1,0:T(4,128)S(1)}, f32[8,4,1024]{2,1,0:T(4,128)S(1)}, ...), condition=%wide.region_12.14_spmd.clone, body=%wide.region_8.13_spmd.clone.sunk | while | flops 9702406 | bytes 77987 | solution.py:82
  73.1 1.9 %fusion.129 = (f32[256]{0:T(256)S(1)}, f32[256]{0:T(256)S(1)}, f32[256]{0:T(256)S(1)}) fusion(f32[1024]{0:T(1024)S(1)} %bitcast.123, f32[256]{0:T(256)S(1)} %bitcast.144, f32[1024]{0:T(1024)S(1)} %bitcast.124, f32[256]{0:T(256)S(1)} %bitcast.143, f32[1024]{0:T(1024)S(1)} %bitcast.122, f32[256]{0:T(256)S(1)} %bitcast.142, f32[1024]{0:T(1024)S(1)} %bitcast.121), kind=kLoop, calls=%fused_computation.48.clone.1 | loop fusion | flops 9698560 | bytes 22528 | tf_op jit(solution)/shard_map/while/body/eval_jaxpr/reduce_sum | solution.py:53
  75.2 1.9 %fusion.129 = (f32[256]{0:T(256)S(1)}, f32[256]{0:T(256)S(1)}, f32[256]{0:T(256)S(1)}) fusion(f32[1024]{0:T(1024)S(1)} %bitcast.123, f32[256]{0:T(256)S(1)} %bitcast.144, f32[1024]{0:T(1024)S(1)} %bitcast.124, f32[256]{0:T(256)S(1)} %bitcast.143, f32[1024]{0:T(1024)S(1)} %bitcast.122, f32[256]{0:T(256)S(1)} %bitcast.142, f32[1024]{0:T(1024)S(1)} %bitcast.121), kind=kLoop, calls=%fused_computation.48.clone.1 | loop fusion | flops 9698560 | bytes 22528 | tf_op jit(solution)/shard_map/while/body/eval_jaxpr/reduce_sum | solution.py:53
  77.2 1.9 %fusion.129 = (f32[256]{0:T(256)S(1)}, f32[256]{0:T(256)S(1)}, f32[256]{0:T(256)S(1)}) fusion(f32[1024]{0:T(1024)S(1)} %bitcast.123, f32[256]{0:T(256)S(1)} %bitcast.144, f32[1024]{0:T(1024)S(1)} %bitcast.124, f32[256]{0:T(256)S(1)} %bitcast.143, f32[1024]{0:T(1024)S(1)} %bitcast.122, f32[256]{0:T(256)S(1)} %bitcast.142, f32[1024]{0:T(1024)S(1)} %bitcast.121), kind=kLoop, calls=%fused_computation.48.clone.1 | loop fusion | flops 9698560 | bytes 22528 | tf_op jit(solution)/shard_map/while/body/eval_jaxpr/reduce_sum | solution.py:53
  79.2 1.9 %fusion.129 = (f32[256]{0:T(256)S(1)}, f32[256]{0:T(256)S(1)}, f32[256]{0:T(256)S(1)}) fusion(f32[1024]{0:T(1024)S(1)} %bitcast.123, f32[256]{0:T(256)S(1)} %bitcast.144, f32[1024]{0:T(1024)S(1)} %bitcast.124, f32[256]{0:T(256)S(1)} %bitcast.143, f32[1024]{0:T(1024)S(1)} %bitcast.122, f32[256]{0:T(256)S(1)} %bitcast.142, f32[1024]{0:T(1024)S(1)} %bitcast.121), kind=kLoop, calls=%fused_computation.48.clone.1 | loop fusion | flops 9698560 | bytes 22528 | tf_op jit(solution)/shard_map/while/body/eval_jaxpr/reduce_sum | solution.py:53
  81.3 1.9 %fusion.129 = (f32[256]{0:T(256)S(1)}, f32[256]{0:T(256)S(1)}, f32[256]{0:T(256)S(1)}) fusion(f32[1024]{0:T(1024)S(1)} %bitcast.123, f32[256]{0:T(256)S(1)} %bitcast.144, f32[1024]{0:T(1024)S(1)} %bitcast.124, f32[256]{0:T(256)S(1)} %bitcast.143, f32[1024]{0:T(1024)S(1)} %bitcast.122, f32[256]{0:T(256)S(1)} %bitcast.142, f32[1024]{0:T(1024)S(1)} %bitcast.121), kind=kLoop, calls=%fused_computation.48.clone.1 | loop fusion | flops 9698560 | bytes 22528 | tf_op jit(solution)/shard_map/while/body/eval_jaxpr/reduce_sum | solution.py:53
  83.3 1.9 %fusion.129 = (f32[256]{0:T(256)S(1)}, f32[256]{0:T(256)S(1)}, f32[256]{0:T(256)S(1)}) fusion(f32[1024]{0:T(1024)S(1)} %bitcast.123, f32[256]{0:T(256)S(1)} %bitcast.144, f32[1024]{0:T(1024)S(1)} %bitcast.124, f32[256]{0:T(256)S(1)} %bitcast.143, f32[1024]{0:T(1024)S(1)} %bitcast.122, f32[256]{0:T(256)S(1)} %bitcast.142, f32[1024]{0:T(1024)S(1)} %bitcast.121), kind=kLoop, calls=%fused_computation.48.clone.1 | loop fusion | flops 9698560 | bytes 22528 | tf_op jit(solution)/shard_map/while/body/eval_jaxpr/reduce_sum | solution.py:53
  85.3 1.9 %fusion.129 = (f32[256]{0:T(256)S(1)}, f32[256]{0:T(256)S(1)}, f32[256]{0:T(256)S(1)}) fusion(f32[1024]{0:T(1024)S(1)} %bitcast.123, f32[256]{0:T(256)S(1)} %bitcast.144, f32[1024]{0:T(1024)S(1)} %bitcast.124, f32[256]{0:T(256)S(1)} %bitcast.143, f32[1024]{0:T(1024)S(1)} %bitcast.122, f32[256]{0:T(256)S(1)} %bitcast.142, f32[1024]{0:T(1024)S(1)} %bitcast.121), kind=kLoop, calls=%fused_computation.48.clone.1 | loop fusion | flops 9698560 | bytes 22528 | tf_op jit(solution)/shard_map/while/body/eval_jaxpr/reduce_sum | solution.py:53
  87.4 1.9 %fusion.129 = (f32[256]{0:T(256)S(1)}, f32[256]{0:T(256)S(1)}, f32[256]{0:T(256)S(1)}) fusion(f32[1024]{0:T(1024)S(1)} %bitcast.123, f32[256]{0:T(256)S(1)} %bitcast.144, f32[1024]{0:T(1024)S(1)} %bitcast.124, f32[256]{0:T(256)S(1)} %bitcast.143, f32[1024]{0:T(1024)S(1)} %bitcast.122, f32[256]{0:T(256)S(1)} %bitcast.142, f32[1024]{0:T(1024)S(1)} %bitcast.121), kind=kLoop, calls=%fused_computation.48.clone.1 | loop fusion | flops 9698560 | bytes 22528 | tf_op jit(solution)/shard_map/while/body/eval_jaxpr/reduce_sum | solution.py:53
  (119 shorter events, 25.8 us)
Async XLA Ops:
  0.6 0.7 copy-start
  2.7 0.7 copy-start.2
  3.4 0.7 copy-start.3
  4.7 5.2 %collective-permute-start = (f32[4,256]{1,0:T(4,128)S(1)}, f32[4,256]{1,0:T(4,128)S(1)}, u32[]{:S(2)}, u32[]{:S(2)}) collective-permute-start(f32[4,256]{1,0:T(4,128)S(1)} %pad_maximum_fusion.5), channel_id=1, source_target_pairs={{0,1},{1,2},{2,3},{3,0},{4,5},{5,6},{6,7},{7,4},{8,9},{9,10},{10,1... | collective-permute-start | bytes 12296 | tf_op jit(solution)/shard_map/ppermute | solution.py:18
  9.9 4.3 %collective-permute-start.1 = (f32[4,256]{1,0:T(4,128)S(1)}, f32[4,256]{1,0:T(4,128)S(1)}, u32[]{:S(2)}, u32[]{:S(2)}) collective-permute-start(f32[4,256]{1,0:T(4,128)S(1)} %collective-permute-done), channel_id=1, source_target_pairs={{0,1},{1,2},{2,3},{3,0},{4,5},{5,6},{6,7},{7,4},{8,9},{9,10},{10,1... | collective-permute-start | bytes 12296 | tf_op jit(solution)/shard_map/ppermute | solution.py:18
  14.2 4.3 %collective-permute-start.2 = (f32[4,256]{1,0:T(4,128)S(1)}, f32[4,256]{1,0:T(4,128)S(1)}, u32[]{:S(2)}, u32[]{:S(2)}) collective-permute-start(f32[4,256]{1,0:T(4,128)S(1)} %collective-permute-done.1), channel_id=1, source_target_pairs={{0,1},{1,2},{2,3},{3,0},{4,5},{5,6},{6,7},{7,4},{8,9},{9,10},{10,1... | collective-permute-start | bytes 12296 | tf_op jit(solution)/shard_map/ppermute | solution.py:18
  18.6 2.9 %collective-permute-start.3 = (f32[4,1024]{1,0:T(4,128)S(1)}, f32[4,1024]{1,0:T(4,128)S(1)}, u32[]{:S(2)}, u32[]{:S(2)}) collective-permute-start(f32[4,1024]{1,0:T(4,128)S(1)} %fusion.100), channel_id=1, source_target_pairs={{4,0},{0,4},{5,1},{1,5},{6,2},{2,6},{7,3},{3,7},{12,8},{8,12},{13,... | collective-permute-start | bytes 49160 | tf_op jit(solution)/shard_map/ppermute | solution.py:27
  21.5 7.1 %collective-permute-start.4 = (f32[2,4,1024]{2,1,0:T(4,128)S(1)}, f32[2,4,1024]{2,1,0:T(4,128)S(1)}, u32[]{:S(2)}, u32[]{:S(2)}) collective-permute-start(f32[2,4,1024]{2,1,0:T(4,128)S(1)} %get-tuple-element.157), channel_id=1, source_target_pairs={{24,0},{0,8},{8,16},{16,24},{25,1},{1,9},{9,17},{17,25},{26,2},{2,... | collective-permute-start | bytes 98312 | tf_op jit(solution)/shard_map/ppermute | solution.py:27
  27.6 2.8 %collective-permute-start.5 = (f32[2,4,1024]{2,1,0:T(4,128)S(1)}, f32[2,4,1024]{2,1,0:T(4,128)S(1)}, u32[]{:S(2)}, u32[]{:S(2)}) collective-permute-start(f32[2,4,1024]{2,1,0:T(4,128)S(1)} %get-tuple-element.157), channel_id=1, source_target_pairs={{16,0},{24,8},{0,16},{8,24},{17,1},{25,9},{1,17},{9,25},{18,2},{26... | collective-permute-start | bytes 98312 | tf_op jit(solution)/shard_map/ppermute | solution.py:27
  27.6 3.3 %collective-permute-start.6 = (f32[2,4,1024]{2,1,0:T(4,128)S(1)}, f32[2,4,1024]{2,1,0:T(4,128)S(1)}, u32[]{:S(2)}, u32[]{:S(2)}) collective-permute-start(f32[2,4,1024]{2,1,0:T(4,128)S(1)} %get-tuple-element.157), channel_id=1, source_target_pairs={{8,0},{16,8},{24,16},{0,24},{9,1},{17,9},{25,17},{1,25},{10,2},{18... | collective-permute-start | bytes 98312 | tf_op jit(solution)/shard_map/ppermute | solution.py:27
  47.3 0.7 copy-start.1
  48.0 4.3 %collective-permute-start.7 = (f32[4,256]{1,0:T(4,128)S(1)}, f32[4,256]{1,0:T(4,128)S(1)}, u32[]{:S(2)}, u32[]{:S(2)}) collective-permute-start(f32[4,256]{1,0:T(4,128)S(1)} %pad_maximum_fusion.4), channel_id=1, source_target_pairs={{0,1},{1,2},{2,3},{3,0},{4,5},{5,6},{6,7},{7,4},{8,9},{9,10},{10,1... | collective-permute-start | bytes 12296 | tf_op jit(solution)/shard_map/ppermute | solution.py:18
  52.3 4.3 %collective-permute-start.8 = (f32[4,256]{1,0:T(4,128)S(1)}, f32[4,256]{1,0:T(4,128)S(1)}, u32[]{:S(2)}, u32[]{:S(2)}) collective-permute-start(f32[4,256]{1,0:T(4,128)S(1)} %collective-permute-done.7), channel_id=1, source_target_pairs={{0,1},{1,2},{2,3},{3,0},{4,5},{5,6},{6,7},{7,4},{8,9},{9,10},{10,1... | collective-permute-start | bytes 12296 | tf_op jit(solution)/shard_map/ppermute | solution.py:18
  56.6 4.3 %collective-permute-start.9 = (f32[4,256]{1,0:T(4,128)S(1)}, f32[4,256]{1,0:T(4,128)S(1)}, u32[]{:S(2)}, u32[]{:S(2)}) collective-permute-start(f32[4,256]{1,0:T(4,128)S(1)} %collective-permute-done.8), channel_id=1, source_target_pairs={{0,1},{1,2},{2,3},{3,0},{4,5},{5,6},{6,7},{7,4},{8,9},{9,10},{10,1... | collective-permute-start | bytes 12296 | tf_op jit(solution)/shard_map/ppermute | solution.py:18
  60.9 2.9 %collective-permute-start.10 = (f32[4,1024]{1,0:T(4,128)S(1)}, f32[4,1024]{1,0:T(4,128)S(1)}, u32[]{:S(2)}, u32[]{:S(2)}) collective-permute-start(f32[4,1024]{1,0:T(4,128)S(1)} %fusion.91), channel_id=1, source_target_pairs={{4,0},{0,4},{5,1},{1,5},{6,2},{2,6},{7,3},{3,7},{12,8},{8,12},{13,... | collective-permute-start | bytes 49160 | tf_op jit(solution)/shard_map/ppermute | solution.py:27
  63.9 6.4 %collective-permute-start.11 = (f32[2,4,1024]{2,1,0:T(4,128)S(1)}, f32[2,4,1024]{2,1,0:T(4,128)S(1)}, u32[]{:S(2)}, u32[]{:S(2)}) collective-permute-start(f32[2,4,1024]{2,1,0:T(4,128)S(1)} %get-tuple-element.155), channel_id=1, source_target_pairs={{24,0},{0,8},{8,16},{16,24},{25,1},{1,9},{9,17},{17,25},{26,2},{2,... | collective-permute-start | bytes 98312 | tf_op jit(solution)/shard_map/ppermute | solution.py:27
  68.9 3.3 %collective-permute-start.12 = (f32[2,4,1024]{2,1,0:T(4,128)S(1)}, f32[2,4,1024]{2,1,0:T(4,128)S(1)}, u32[]{:S(2)}, u32[]{:S(2)}) collective-permute-start(f32[2,4,1024]{2,1,0:T(4,128)S(1)} %get-tuple-element.155), channel_id=1, source_target_pairs={{16,0},{24,8},{0,16},{8,24},{17,1},{25,9},{1,17},{9,25},{18,2},{26... | collective-permute-start | bytes 98312 | tf_op jit(solution)/shard_map/ppermute | solution.py:27
  69.7 3.3 %collective-permute-start.13 = (f32[2,4,1024]{2,1,0:T(4,128)S(1)}, f32[2,4,1024]{2,1,0:T(4,128)S(1)}, u32[]{:S(2)}, u32[]{:S(2)}) collective-permute-start(f32[2,4,1024]{2,1,0:T(4,128)S(1)} %get-tuple-element.155), channel_id=1, source_target_pairs={{8,0},{16,8},{24,16},{0,24},{9,1},{17,9},{25,17},{1,25},{10,2},{18... | collective-permute-start | bytes 98312 | tf_op jit(solution)/shard_map/ppermute | solution.py:27
